TPU v7x, 1024 devices: a whole 4x4x32 slice. The times are simulated.
1024 devices in a mesh: gx: 8 (over z_lo), gy: 32 (over y, z_hi, core), gz: 4 (over x).
Axes of the slice: x: 4, y: 4, z: 32 (z_hi: 4, z_lo: 8; z = z_hi * 8 + z_lo), core: 2. Of those that a mesh axis runs over, the one named last changes fastest.
Arguments:
- positions: float32 [8, 32, 4, 3, 32, 128], P('gx', 'gy', 'gz'), may hold values from 0 to 1
- velocities: float32 [8, 32, 4, 3, 32, 128], P('gx', 'gy', 'gz'), may hold values from -6 to 6
- strength: float32 [8, 32, 4, 32, 128], P('gx', 'gy', 'gz'), may hold values from 0.5 to 2
- tower_slots: int32 [8, 32, 4, 128], P('gx', 'gy', 'gz'), may hold values from 0 to 159
- plate_slots: int32 [8, 32, 4, 128], P('gx', 'gy', 'gz'), may hold values from 0 to 383
- pair_count: int32 [8, 32, 4], P('gx', 'gy', 'gz'), may hold values from 16 to 128, as said below
Outputs:
- new_positions: float32 [8, 32, 4, 3, 32, 128], P('gx', 'gy', 'gz')
- new_velocities: float32 [8, 32, 4, 3, 32, 128], P('gx', 'gy', 'gz')
Inputs may be any that keep to these rules, and one draw needn't show every extreme that they name: `pair_count`: slots at or beyond a device's count are padding. Some device has all 128 slots in use.
All inputs are finite; a program needn't handle non-finite values.
Results may differ from a plain program's by a relative error of at most 0.0003.
Values sent between devices are 32-bit elements; how exact they have to be, the bound alone decides.
A program may use at most 32 MiB of HBM per device.

v0:
```python
import math

import jax
import jax.numpy as jnp
from jax import lax
from jax.sharding import PartitionSpec as P

time_step = 0.02
cutoff_sq = 4.0
repulsion = 4.0
pair_block = 16


def from_behind(value, axis, steps):
    count = lax.axis_size(axis)
    pairs = [(source, (source + steps) % count) for source in range(count)]
    return lax.ppermute(value, axis, pairs)


def in_one_piece(arrays, axis, dim, along):
    widths = [math.prod(a.shape[along:]) for a in arrays]
    both = jnp.concatenate(
        [a.reshape(*a.shape[:along], w) for a, w in zip(arrays, widths)], axis=along
    )
    result = lax.all_gather(both, axis, axis=dim, tiled=True)
    blocks = jnp.split(result, [sum(widths[:k]) for k in range(1, len(widths))], axis=along)
    return tuple(
        (b.reshape(*result.shape[:along], *a.shape[along:]) for a, b in zip(arrays, blocks))
    )


def in_blocks(value, dim, count):
    before, after = (value.shape[:dim], value.shape[dim + 1 :])
    return jnp.moveaxis(value.reshape(*before, count, -1, *after), dim, 0)


def summed_on_arrival(value, axis, dim):
    count = lax.axis_size(axis)
    blocks = lax.all_to_all(in_blocks(value, dim, count), axis, 0, 0, tiled=True)
    return jnp.sum(blocks, axis=0)


def row_move(payload, offset):
    return from_behind(payload, "gx", offset)


def line_move(payload, offset):
    return from_behind(payload, "gy", offset)


def height_collect(payload):
    return in_one_piece((payload[0], payload[1]), "gz", 1, 2)


def height_reduce(payload):
    return summed_on_arrival(payload, "gz", 1)


def line_import(payload):
    return [payload, line_move(payload, -1), line_move(payload, -2)]


def line_return(force_parts):
    return force_parts[0] + line_move(force_parts[1], 1) + line_move(force_parts[2], 2)


def placed_tower(tower_pos, height_level):
    shifts = (jnp.arange(5, dtype=jnp.float32) - 2.0)[:, None, None]
    return jnp.stack(
        [tower_pos[:, 0] + shifts, tower_pos[:, 1], tower_pos[:, 2] + height_level], axis=1
    )


def placed_plate(plate_pos):
    line_shift = jnp.arange(plate_pos.shape[0], dtype=jnp.float32)[:, None, None, None]
    height_shift = jnp.arange(plate_pos.shape[1], dtype=jnp.float32)[None, :, None, None]
    return jnp.stack(
        [plate_pos[:, :, 0], plate_pos[:, :, 1] + line_shift, plate_pos[:, :, 2] + height_shift],
        axis=2,
    )


def block_forces(
    accum, begin_at, tower_pos, tower_str, plate_pos, plate_str, tower_list, plate_list, pair_total
):
    tower_force, plate_force = accum
    clusters = tower_pos.shape[2]
    tower_pick = lax.dynamic_slice_in_dim(tower_list, begin_at, pair_block)
    plate_pick = lax.dynamic_slice_in_dim(plate_list, begin_at, pair_block)
    tower_block = tower_pick // clusters
    tower_index = tower_pick % clusters
    plate_block = plate_pick // clusters
    plate_index = plate_pick % clusters
    tower_side = tower_pos[tower_block, :, tower_index, :]
    plate_side = plate_pos[plate_block, :, plate_index, :]
    tower_weight = tower_str[tower_block, tower_index]
    plate_weight = plate_str[plate_block, plate_index]
    live_mask = (begin_at + jnp.arange(pair_block, dtype=jnp.int32) < pair_total).astype(
        jnp.float32
    )
    separation = tower_side[:, :, :, None] - plate_side[:, :, None, :]
    dist_sq = jnp.sum(separation * separation, axis=1)
    softness = jnp.maximum(1.0 - dist_sq / cutoff_sq, 0.0)
    weight = (
        repulsion
        * softness
        * softness
        * tower_weight[:, :, None]
        * plate_weight[:, None, :]
        * live_mask[:, None, None]
    )
    pair_push = weight[:, None] * separation
    tower_force = tower_force.at[tower_block, :, tower_index, :].add(jnp.sum(pair_push, axis=3))
    plate_force = plate_force.at[plate_block, :, plate_index, :].add(-jnp.sum(pair_push, axis=2))
    return (tower_force, plate_force)


def total_force(coords, weights, tower_list, plate_list, pair_total, height_level):
    tower_parts = []
    for offset in (-2, -1, 0, 1, 2):
        if offset == 0:
            tower_parts.append((coords, weights))
        else:
            tower_parts.append(row_move((coords, weights), -offset))
    tower_pos = placed_tower(jnp.stack([piece[0] for piece in tower_parts]), height_level)
    tower_str = jnp.stack([piece[1] for piece in tower_parts])
    own_block = (coords[None, None], weights[None, None])
    line_list = line_import(own_block)
    plate_pos, plate_str = height_collect(
        (
            jnp.concatenate([piece[0] for piece in line_list], axis=0),
            jnp.concatenate([piece[1] for piece in line_list], axis=0),
        )
    )
    heights_total = plate_pos.shape[1]
    plate_flat = placed_plate(plate_pos).reshape((3 * heights_total,) + plate_pos.shape[2:])
    plate_str_flat = plate_str.reshape((3 * heights_total,) + plate_str.shape[2:])
    start_force = (
        jnp.zeros(tower_pos.shape, jnp.float32),
        jnp.zeros(plate_flat.shape, jnp.float32),
    )

    def advance(block_id, state):
        return block_forces(
            state,
            block_id * pair_block,
            tower_pos,
            tower_str,
            plate_flat,
            plate_str_flat,
            tower_list,
            plate_list,
            pair_total,
        )

    live_blocks = (pair_total + pair_block - 1) // pair_block
    tower_force, plate_force = lax.fori_loop(0, live_blocks, advance, start_force)
    combined = tower_force[2]
    for offset in (-2, -1, 1, 2):
        combined = combined + row_move(tower_force[offset + 2], offset)
    plate_force = plate_force.reshape((3, heights_total) + plate_pos.shape[2:])
    reduced = height_reduce(plate_force)
    returned = line_return([reduced[0:1], reduced[1:2], reduced[2:3]])
    return combined + returned[0, 0]


def shards(positions, velocities, strength, tower_slots, plate_slots, pair_count):
    coords = positions[0, 0, 0]
    speeds = velocities[0, 0, 0]
    weights = strength[0, 0, 0]
    tower_list = tower_slots[0, 0, 0]
    plate_list = plate_slots[0, 0, 0]
    pair_total = pair_count[0, 0, 0]
    height_level = lax.axis_index("gz").astype(jnp.float32)
    for leap_index in range(2):
        force = total_force(coords, weights, tower_list, plate_list, pair_total, height_level)
        speeds = speeds + time_step * force
        coords = coords + time_step * speeds
    return (coords[None, None, None], speeds[None, None, None])


def solution(mesh):
    in_specs = (
        P("gx", "gy", "gz", None, None, None),
        P("gx", "gy", "gz", None, None, None),
        P("gx", "gy", "gz", None, None),
        P("gx", "gy", "gz", None),
        P("gx", "gy", "gz", None),
        P("gx", "gy", "gz"),
    )
    out_specs = (P("gx", "gy", "gz", None, None, None), P("gx", "gy", "gz", None, None, None))
    return jax.shard_map(shards, mesh=mesh, in_specs=in_specs, out_specs=out_specs, check_vma=False)
```

profile of v0, /device:TPU:71, one launch (start us, length us, event | category | flops | bytes accessed | tf_op | source)
XLA Modules:
  0.0 436.7 jit_solution(15656438273546353921)
XLA Ops:
  0.6 2.6 collective-permute-start.6
  3.2 23.4 %collective-permute-start.7 = (f32[1,1,32,128]{3,2,1,0:T(8,128)}, f32[1,1,32,128]{3,2,1,0:T(8,128)S(1)}, u32[]{:S(2)}, u32[]{:S(2)}) collective-permute-start(f32[1,1,32,128]{3,2,1,0:T(8,128)} %bitcast.312), channel_id=1, source_target_pairs={{0,120},{4,124},{8,0},{12,4},{16,8},{20,12},{24,16},{28,20},{32,24... | collective-permute-start | bytes 49160 | tf_op jit(solution)/shard_map/ppermute | solution.py:17
  26.6 8.2 %collective-permute-start.4 = (f32[1,1,3,32,128]{4,3,2,1,0:T(8,128)}, f32[1,1,3,32,128]{4,3,2,1,0:T(8,128)S(1)}, u32[]{:S(2)}, u32[]{:S(2)}) collective-permute-start(f32[1,1,3,32,128]{4,3,2,1,0:T(8,128)} %bitcast.298), channel_id=1, source_target_pairs={{0,124},{4,0},{8,4},{12,8},{16,12},{20,16},{24,20},{28,24},{32,28}... | collective-permute-start | bytes 147464 | tf_op jit(solution)/shard_map/ppermute | solution.py:17
  34.8 2.2 collective-permute-start.5
  37.8 4.3 collective-permute-start
  42.8 3.5 collective-permute-start.1
  46.4 4.9 %collective-permute-start.8 = (f32[32,128]{1,0:T(8,128)}, f32[32,128]{1,0:T(8,128)S(1)}, u32[]{:S(2)}, u32[]{:S(2)}) collective-permute-start(f32[32,128]{1,0:T(8,128)} %bitcast.313), channel_id=1, source_target_pairs={{0,256},{128,384},{256,512},{384,640},{512,768},{640,896},{768,0},... | collective-permute-start | bytes 49160 | tf_op jit(solution)/shard_map/ppermute | solution.py:17
  52.3 3.5 collective-permute-start.9
  55.8 6.0 %collective-permute-done.9 = f32[32,128]{1,0:T(8,128)S(1)} collective-permute-done((f32[32,128]{1,0:T(8,128)}, f32[32,128]{1,0:T(8,128)S(1)}, u32[]{:S(2)}, u32[]{:S(2)}) %collective-permute-start.9) | collective-permute-done | bytes 16416 | tf_op jit(solution)/shard_map/ppermute | solution.py:17
  61.8 3.6 collective-permute-start.10
  66.5 11.4 %collective-permute-start.11 = (f32[32,128]{1,0:T(8,128)}, f32[32,128]{1,0:T(8,128)S(1)}, u32[]{:S(2)}, u32[]{:S(2)}) collective-permute-start(f32[32,128]{1,0:T(8,128)} %bitcast.317), channel_id=1, source_target_pairs={{0,768},{128,896},{256,0},{384,128},{512,256},{640,384},{768,512},... | collective-permute-start | bytes 49160 | tf_op jit(solution)/shard_map/ppermute | solution.py:17
  78.9 7.6 %collective-permute-start.2 = (f32[3,32,128]{2,0,1:T(4,128)S(1)}, f32[3,32,128]{2,0,1:T(4,128)S(1)}, u32[]{:S(2)}, u32[]{:S(2)}) collective-permute-start(f32[3,32,128]{2,0,1:T(4,128)S(1)} %bitcast.321), channel_id=1, source_target_pairs={{0,896},{128,0},{256,128},{384,256},{512,384},{640,512},{768,640},... | collective-permute-start | bytes 147464 | tf_op jit(solution)/shard_map/ppermute | solution.py:17
  86.6 10.2 %collective-permute-start.3 = (f32[3,32,128]{2,0,1:T(4,128)S(1)}, f32[3,32,128]{2,0,1:T(4,128)S(1)}, u32[]{:S(2)}, u32[]{:S(2)}) collective-permute-start(f32[3,32,128]{2,0,1:T(4,128)S(1)} %bitcast.322), channel_id=1, source_target_pairs={{0,768},{128,896},{256,0},{384,128},{512,256},{640,384},{768,512},... | collective-permute-start | bytes 147464 | tf_op jit(solution)/shard_map/ppermute | solution.py:17
  97.8 12.3 %all_gather.6 = f32[3,4,16384]{2,0,1:T(4,128)S(1)} all-gather(f32[3,1,16384]{2,0,1:T(4,128)S(1)} %pad_maximum_fusion.4), channel_id=1, replica_groups=mesh['gx'=8,'gy'=32,'gz'=4] {'gz'}, dimensions={1}, use_global_device_ids=true | all-gather | bytes 983040 | tf_op jit(solution)/shard_map/all_gather | solution.py:25
  113.9 41.3 %while.30 = (s32[]{:T(128)}, f32[5,3,32,128]{3,1,2,0:T(4,128)S(1)}, f32[12,3,32,128]{3,1,2,0:T(4,128)S(1)}, s32[]{:T(128)}, s32[128]{0:T(128)S(1)}, /*index=5*/f...) while((s32[]{:T(128)}, f32[5,3,32,128]{3,1,2,0:T(4,128)S(1)}, ...), condition=%wide.region_6.7_spmd, body=%wide.region_0.6_spmd.sunk | while | flops 7347318 | bytes 4687303 | solution.py:157
  114.7 1.6 gather_fusion.1
  119.6 2.1 fusion.68
  121.7 1.3 scatter_fusion.1
  123.0 1.3 scatter_fusion
  125.0 1.6 gather_fusion.1
  129.9 2.1 fusion.68
  132.0 1.3 scatter_fusion.1
  133.3 1.3 scatter_fusion
  135.3 1.6 gather_fusion.1
  140.2 2.1 fusion.68
  142.3 1.3 scatter_fusion.1
  143.6 1.3 scatter_fusion
  145.6 1.6 gather_fusion.1
  150.5 2.1 fusion.68
  156.2 3.9 all-to-all-start
  160.2 41.9 %collective-permute-start.12 = (f32[3,32,128]{2,0,1:T(4,128)S(1)}, f32[3,32,128]{2,0,1:T(4,128)S(1)}, u32[]{:S(2)}, u32[]{:S(2)}) collective-permute-start(f32[3,32,128]{2,0,1:T(4,128)S(1)} %get-tuple-element.469), channel_id=1, source_target_pairs={{0,768},{128,896},{256,0},{384,128},{512,256},{640,384},{768,512},... | collective-permute-start | bytes 147464 | tf_op jit(solution)/shard_map/ppermute | solution.py:17
  202.1 2.0 collective-permute-start.13
  204.1 3.3 collective-permute-start.14
  207.4 4.1 collective-permute-start.15
  211.6 19.7 %collective-permute-start.16 = (f32[1,1,3,32,128]{4,2,3,1,0:T(4,128)S(1)}, f32[1,1,3,32,128]{4,2,3,1,0:T(4,128)S(1)}, u32[]{:S(2)}, u32[]{:S(2)}) collective-permute-start(f32[1,1,3,32,128]{4,2,3,1,0:T(4,128)S(1)} %bitcast.323), channel_id=1, source_target_pairs={{0,4},{4,8},{8,12},{12,16},{16,20},{20,24},{24,28},{28,32},{32,36}... | collective-permute-start | bytes 147464 | tf_op jit(solution)/shard_map/ppermute | solution.py:17
  231.4 1.9 collective-permute-start.17
  233.4 5.3 %collective-permute-done.16 = f32[1,1,3,32,128]{4,2,3,1,0:T(4,128)S(1)} collective-permute-done((f32[1,1,3,32,128]{4,2,3,1,0:T(4,128)S(1)}, f32[1,1,3,32,128]{4,2,3,1,0:T(4,128)S(1)}, u32[]{:S(2)}, u32[]{:S(2)}) %collective-permute-start.16) | collective-permute-done | bytes 49184 | tf_op jit(solution)/shard_map/ppermute | solution.py:17
  238.7 12.4 %collective-permute-done.17 = f32[1,1,3,32,128]{4,2,3,1,0:T(4,128)S(1)} collective-permute-done((f32[1,1,3,32,128]{4,2,3,1,0:T(4,128)S(1)}, f32[1,1,3,32,128]{4,2,3,1,0:T(4,128)S(1)}, u32[]{:S(2)}, u32[]{:S(2)}) %collective-permute-start.17) | collective-permute-done | bytes 49184 | tf_op jit(solution)/shard_map/ppermute | solution.py:17
  251.3 1.9 collective-permute-start.22
  253.2 3.8 collective-permute-start.23
  257.0 1.9 collective-permute-start.18
  258.9 1.9 collective-permute-start.19
  260.9 3.4 collective-permute-start.20
  264.2 17.9 %collective-permute-done.22 = f32[1,1,3,32,128]{4,2,3,1,0:T(4,128)S(1)} collective-permute-done((f32[1,1,3,32,128]{4,2,3,1,0:T(4,128)S(1)}, f32[1,1,3,32,128]{4,2,3,1,0:T(4,128)S(1)}, u32[]{:S(2)}, u32[]{:S(2)}) %collective-permute-start.22) | collective-permute-done | bytes 49184 | tf_op jit(solution)/shard_map/ppermute | solution.py:17
  282.1 1.9 collective-permute-start.21
  284.4 11.7 %all_gather.7 = f32[3,4,16384]{2,0,1:T(4,128)S(1)} all-gather(f32[3,1,16384]{2,0,1:T(4,128)S(1)} %copy.100), channel_id=1, replica_groups=mesh['gx'=8,'gy'=32,'gz'=4] {'gz'}, dimensions={1}, use_global_device_ids=true | all-gather | bytes 983040 | tf_op jit(solution)/shard_map/all_gather | solution.py:25
  299.2 41.5 %while.31 = (s32[]{:T(128)}, f32[5,3,32,128]{3,1,2,0:T(4,128)S(1)}, f32[12,3,32,128]{3,1,2,0:T(4,128)S(1)}, s32[]{:T(128)}, s32[128]{0:T(128)S(1)}, /*index=5*/f...) while((s32[]{:T(128)}, f32[5,3,32,128]{3,1,2,0:T(4,128)S(1)}, ...), condition=%wide.region_14.15_spmd, body=%wide.region_8.14_spmd.sunk | while | flops 7347318 | bytes 4687303 | solution.py:157
  300.2 1.6 gather_fusion.5
  305.1 2.1 fusion.72
  310.5 1.6 gather_fusion.5
  315.4 2.1 fusion.72
  320.8 1.6 gather_fusion.5
  325.7 2.1 fusion.72
  329.1 1.3 scatter_fusion.2
  331.1 1.6 gather_fusion.5
  336.0 2.1 fusion.72
  341.7 5.0 %all-to-all-start.1 = ((f32[4,3,1,3,32,128]{5,4,3,2,1,0:T(8,128)}), f32[4,3,1,3,32,128]{5,4,3,2,1,0:T(8,128)S(1)}, u32[]{:S(2)}, u32[]{:S(2)}) async-start(f32[4,3,1,3,32,128]{5,4,3,2,1,0:T(8,128)} %copy.107), calls=%async_computation.1 | async-start | bytes 1179648 | tf_op jit(solution)/shard_map/all_to_all | solution.py:39
  346.7 33.6 %collective-permute-start.24 = (f32[3,32,128]{2,0,1:T(4,128)S(1)}, f32[3,32,128]{2,0,1:T(4,128)S(1)}, u32[]{:S(2)}, u32[]{:S(2)}) collective-permute-start(f32[3,32,128]{2,0,1:T(4,128)S(1)} %get-tuple-element.462), channel_id=1, source_target_pairs={{0,768},{128,896},{256,0},{384,128},{512,256},{640,384},{768,512},... | collective-permute-start | bytes 147464 | tf_op jit(solution)/shard_map/ppermute | solution.py:17
  380.4 4.6 %collective-permute-start.25 = (f32[3,32,128]{2,0,1:T(4,128)S(1)}, f32[3,32,128]{2,0,1:T(4,128)S(1)}, u32[]{:S(2)}, u32[]{:S(2)}) collective-permute-start(f32[3,32,128]{2,0,1:T(4,128)S(1)} %get-tuple-element.465), channel_id=1, source_target_pairs={{0,896},{128,0},{256,128},{384,256},{512,384},{640,512},{768,640},... | collective-permute-start | bytes 147464 | tf_op jit(solution)/shard_map/ppermute | solution.py:17
  384.9 5.0 %collective-permute-start.26 = (f32[3,32,128]{2,0,1:T(4,128)S(1)}, f32[3,32,128]{2,0,1:T(4,128)S(1)}, u32[]{:S(2)}, u32[]{:S(2)}) collective-permute-start(f32[3,32,128]{2,0,1:T(4,128)S(1)} %get-tuple-element.464), channel_id=1, source_target_pairs={{0,128},{128,256},{256,384},{384,512},{512,640},{640,768},{768,896... | collective-permute-start | bytes 147464 | tf_op jit(solution)/shard_map/ppermute | solution.py:17
  389.9 9.7 %collective-permute-start.27 = (f32[3,32,128]{2,0,1:T(4,128)S(1)}, f32[3,32,128]{2,0,1:T(4,128)S(1)}, u32[]{:S(2)}, u32[]{:S(2)}) collective-permute-start(f32[3,32,128]{2,0,1:T(4,128)S(1)} %get-tuple-element.463), channel_id=1, source_target_pairs={{0,256},{128,384},{256,512},{384,640},{512,768},{640,896},{768,0},... | collective-permute-start | bytes 147464 | tf_op jit(solution)/shard_map/ppermute | solution.py:17
  399.8 10.4 %collective-permute-start.28 = (f32[1,1,3,32,128]{4,2,3,1,0:T(4,128)S(1)}, f32[1,1,3,32,128]{4,2,3,1,0:T(4,128)S(1)}, u32[]{:S(2)}, u32[]{:S(2)}) collective-permute-start(f32[1,1,3,32,128]{4,2,3,1,0:T(4,128)S(1)} %bitcast.324), channel_id=1, source_target_pairs={{0,4},{4,8},{8,12},{12,16},{16,20},{20,24},{24,28},{28,32},{32,36}... | collective-permute-start | bytes 147464 | tf_op jit(solution)/shard_map/ppermute | solution.py:17
  410.2 6.4 %collective-permute-start.29 = (f32[1,1,3,32,128]{4,2,3,1,0:T(4,128)S(1)}, f32[1,1,3,32,128]{4,2,3,1,0:T(4,128)S(1)}, u32[]{:S(2)}, u32[]{:S(2)}) collective-permute-start(f32[1,1,3,32,128]{4,2,3,1,0:T(4,128)S(1)} %bitcast.326), channel_id=1, source_target_pairs={{0,8},{4,12},{8,16},{12,20},{16,24},{20,28},{24,32},{28,36},{32,40... | collective-permute-start | bytes 147464 | tf_op jit(solution)/shard_map/ppermute | solution.py:17
  416.7 18.7 %collective-permute-done.29 = f32[1,1,3,32,128]{4,2,3,1,0:T(4,128)S(1)} collective-permute-done((f32[1,1,3,32,128]{4,2,3,1,0:T(4,128)S(1)}, f32[1,1,3,32,128]{4,2,3,1,0:T(4,128)S(1)}, u32[]{:S(2)}, u32[]{:S(2)}) %collective-permute-start.29) | collective-permute-done | bytes 49184 | tf_op jit(solution)/shard_map/ppermute | solution.py:17
  (180 shorter events, 59.5 us)
Async XLA Ops:
  0.6 42.2 %collective-permute-start.6 = (f32[1,1,32,128]{3,2,1,0:T(8,128)}, f32[1,1,32,128]{3,2,1,0:T(8,128)S(1)}, u32[]{:S(2)}, u32[]{:S(2)}) collective-permute-start(f32[1,1,32,128]{3,2,1,0:T(8,128)} %bitcast.311), channel_id=1, source_target_pairs={{0,124},{4,0},{8,4},{12,8},{16,12},{20,16},{24,20},{28,24},{32,28}... | collective-permute-start | bytes 49160 | tf_op jit(solution)/shard_map/ppermute | solution.py:17
  3.2 43.1 %collective-permute-start.7 = (f32[1,1,32,128]{3,2,1,0:T(8,128)}, f32[1,1,32,128]{3,2,1,0:T(8,128)S(1)}, u32[]{:S(2)}, u32[]{:S(2)}) collective-permute-start(f32[1,1,32,128]{3,2,1,0:T(8,128)} %bitcast.312), channel_id=1, source_target_pairs={{0,120},{4,124},{8,0},{12,4},{16,8},{20,12},{24,16},{28,20},{32,24... | collective-permute-start | bytes 49160 | tf_op jit(solution)/shard_map/ppermute | solution.py:17
  26.6 60.0 %collective-permute-start.4 = (f32[1,1,3,32,128]{4,3,2,1,0:T(8,128)}, f32[1,1,3,32,128]{4,3,2,1,0:T(8,128)S(1)}, u32[]{:S(2)}, u32[]{:S(2)}) collective-permute-start(f32[1,1,3,32,128]{4,3,2,1,0:T(8,128)} %bitcast.298), channel_id=1, source_target_pairs={{0,124},{4,0},{8,4},{12,8},{16,12},{20,16},{24,20},{28,24},{32,28}... | collective-permute-start | bytes 147464 | tf_op jit(solution)/shard_map/ppermute | solution.py:17
  34.8 62.1 %collective-permute-start.5 = (f32[1,1,3,32,128]{4,3,2,1,0:T(8,128)}, f32[1,1,3,32,128]{4,3,2,1,0:T(8,128)S(1)}, u32[]{:S(2)}, u32[]{:S(2)}) collective-permute-start(f32[1,1,3,32,128]{4,3,2,1,0:T(8,128)} %bitcast.299), channel_id=1, source_target_pairs={{0,120},{4,124},{8,0},{12,4},{16,8},{20,12},{24,16},{28,20},{32,24... | collective-permute-start | bytes 147464 | tf_op jit(solution)/shard_map/ppermute | solution.py:17
  37.8 72.9 %collective-permute-start = (f32[3,32,128]{2,0,1:T(4,128)S(1)}, f32[3,32,128]{2,0,1:T(4,128)S(1)}, u32[]{:S(2)}, u32[]{:S(2)}) collective-permute-start(f32[3,32,128]{2,0,1:T(4,128)S(1)} %bitcast.319), channel_id=1, source_target_pairs={{0,256},{128,384},{256,512},{384,640},{512,768},{640,896},{768,0},... | collective-permute-start | bytes 147464 | tf_op jit(solution)/shard_map/ppermute | solution.py:17
  42.8 68.0 %collective-permute-start.1 = (f32[3,32,128]{2,0,1:T(4,128)S(1)}, f32[3,32,128]{2,0,1:T(4,128)S(1)}, u32[]{:S(2)}, u32[]{:S(2)}) collective-permute-start(f32[3,32,128]{2,0,1:T(4,128)S(1)} %bitcast.320), channel_id=1, source_target_pairs={{0,128},{128,256},{256,384},{384,512},{512,640},{640,768},{768,896... | collective-permute-start | bytes 147464 | tf_op jit(solution)/shard_map/ppermute | solution.py:17
  46.4 6.0 %collective-permute-start.8 = (f32[32,128]{1,0:T(8,128)}, f32[32,128]{1,0:T(8,128)S(1)}, u32[]{:S(2)}, u32[]{:S(2)}) collective-permute-start(f32[32,128]{1,0:T(8,128)} %bitcast.313), channel_id=1, source_target_pairs={{0,256},{128,384},{256,512},{384,640},{512,768},{640,896},{768,0},... | collective-permute-start | bytes 49160 | tf_op jit(solution)/shard_map/ppermute | solution.py:17
  52.3 9.4 %collective-permute-start.9 = (f32[32,128]{1,0:T(8,128)}, f32[32,128]{1,0:T(8,128)S(1)}, u32[]{:S(2)}, u32[]{:S(2)}) collective-permute-start(f32[32,128]{1,0:T(8,128)} %bitcast.315), channel_id=1, source_target_pairs={{0,128},{128,256},{256,384},{384,512},{512,640},{640,768},{768,896... | collective-permute-start | bytes 49160 | tf_op jit(solution)/shard_map/ppermute | solution.py:17
  61.8 4.7 %collective-permute-start.10 = (f32[32,128]{1,0:T(8,128)}, f32[32,128]{1,0:T(8,128)S(1)}, u32[]{:S(2)}, u32[]{:S(2)}) collective-permute-start(f32[32,128]{1,0:T(8,128)} %bitcast.316), channel_id=1, source_target_pairs={{0,896},{128,0},{256,128},{384,256},{512,384},{640,512},{768,640},... | collective-permute-start | bytes 49160 | tf_op jit(solution)/shard_map/ppermute | solution.py:17
  66.5 12.4 %collective-permute-start.11 = (f32[32,128]{1,0:T(8,128)}, f32[32,128]{1,0:T(8,128)S(1)}, u32[]{:S(2)}, u32[]{:S(2)}) collective-permute-start(f32[32,128]{1,0:T(8,128)} %bitcast.317), channel_id=1, source_target_pairs={{0,768},{128,896},{256,0},{384,128},{512,256},{640,384},{768,512},... | collective-permute-start | bytes 49160 | tf_op jit(solution)/shard_map/ppermute | solution.py:17
  78.9 32.6 %collective-permute-start.2 = (f32[3,32,128]{2,0,1:T(4,128)S(1)}, f32[3,32,128]{2,0,1:T(4,128)S(1)}, u32[]{:S(2)}, u32[]{:S(2)}) collective-permute-start(f32[3,32,128]{2,0,1:T(4,128)S(1)} %bitcast.321), channel_id=1, source_target_pairs={{0,896},{128,0},{256,128},{384,256},{512,384},{640,512},{768,640},... | collective-permute-start | bytes 147464 | tf_op jit(solution)/shard_map/ppermute | solution.py:17
  86.6 25.9 %collective-permute-start.3 = (f32[3,32,128]{2,0,1:T(4,128)S(1)}, f32[3,32,128]{2,0,1:T(4,128)S(1)}, u32[]{:S(2)}, u32[]{:S(2)}) collective-permute-start(f32[3,32,128]{2,0,1:T(4,128)S(1)} %bitcast.322), channel_id=1, source_target_pairs={{0,768},{128,896},{256,0},{384,128},{512,256},{640,384},{768,512},... | collective-permute-start | bytes 147464 | tf_op jit(solution)/shard_map/ppermute | solution.py:17
  110.7 0.8 copy-start
  112.5 1.4 copy-start.2
  112.5 1.4 copy-start.3
  156.2 55.3 %all-to-all-start = ((f32[4,3,1,3,32,128]{5,4,3,2,1,0:T(8,128)}), f32[4,3,1,3,32,128]{5,4,3,2,1,0:T(8,128)S(1)}, u32[]{:S(2)}, u32[]{:S(2)}) async-start(f32[4,3,1,3,32,128]{5,4,3,2,1,0:T(8,128)} %copy.95), calls=%async_computation | async-start | bytes 1179648 | tf_op jit(solution)/shard_map/all_to_all | solution.py:39
  160.1 91.0 %copy-start.4 = (f32[1,1,1,3,32,128]{5,4,3,2,1,0:T(8,128)S(1)}, f32[1,1,1,3,32,128]{5,4,3,2,1,0:T(8,128)}, u32[]{:S(2)}) copy-start(f32[1,1,1,3,32,128]{5,4,3,2,1,0:T(8,128)} %param.11) | copy-start | bytes 147460
  160.2 71.3 %collective-permute-start.12 = (f32[3,32,128]{2,0,1:T(4,128)S(1)}, f32[3,32,128]{2,0,1:T(4,128)S(1)}, u32[]{:S(2)}, u32[]{:S(2)}) collective-permute-start(f32[3,32,128]{2,0,1:T(4,128)S(1)} %get-tuple-element.469), channel_id=1, source_target_pairs={{0,768},{128,896},{256,0},{384,128},{512,256},{640,384},{768,512},... | collective-permute-start | bytes 147464 | tf_op jit(solution)/shard_map/ppermute | solution.py:17
  202.1 31.3 %collective-permute-start.13 = (f32[3,32,128]{2,0,1:T(4,128)S(1)}, f32[3,32,128]{2,0,1:T(4,128)S(1)}, u32[]{:S(2)}, u32[]{:S(2)}) collective-permute-start(f32[3,32,128]{2,0,1:T(4,128)S(1)} %get-tuple-element.472), channel_id=1, source_target_pairs={{0,896},{128,0},{256,128},{384,256},{512,384},{640,512},{768,640},... | collective-permute-start | bytes 147464 | tf_op jit(solution)/shard_map/ppermute | solution.py:17
  204.1 29.3 %collective-permute-start.14 = (f32[3,32,128]{2,0,1:T(4,128)S(1)}, f32[3,32,128]{2,0,1:T(4,128)S(1)}, u32[]{:S(2)}, u32[]{:S(2)}) collective-permute-start(f32[3,32,128]{2,0,1:T(4,128)S(1)} %get-tuple-element.471), channel_id=1, source_target_pairs={{0,128},{128,256},{256,384},{384,512},{512,640},{640,768},{768,896... | collective-permute-start | bytes 147464 | tf_op jit(solution)/shard_map/ppermute | solution.py:17
  207.4 76.7 %copy-start.1 = (f32[1,1,1,32,128]{4,3,2,1,0:T(8,128)S(1)}, f32[1,1,1,32,128]{4,3,2,1,0:T(8,128)}, u32[]{:S(2)}) copy-start(f32[1,1,1,32,128]{4,3,2,1,0:T(8,128)} %param.12) | copy-start | bytes 49156
  207.4 26.0 %collective-permute-start.15 = (f32[3,32,128]{2,0,1:T(4,128)S(1)}, f32[3,32,128]{2,0,1:T(4,128)S(1)}, u32[]{:S(2)}, u32[]{:S(2)}) collective-permute-start(f32[3,32,128]{2,0,1:T(4,128)S(1)} %get-tuple-element.470), channel_id=1, source_target_pairs={{0,256},{128,384},{256,512},{384,640},{512,768},{640,896},{768,0},... | collective-permute-start | bytes 147464 | tf_op jit(solution)/shard_map/ppermute | solution.py:17
  211.6 27.1 %collective-permute-start.16 = (f32[1,1,3,32,128]{4,2,3,1,0:T(4,128)S(1)}, f32[1,1,3,32,128]{4,2,3,1,0:T(4,128)S(1)}, u32[]{:S(2)}, u32[]{:S(2)}) collective-permute-start(f32[1,1,3,32,128]{4,2,3,1,0:T(4,128)S(1)} %bitcast.323), channel_id=1, source_target_pairs={{0,4},{4,8},{8,12},{12,16},{16,20},{20,24},{24,28},{28,32},{32,36}... | collective-permute-start | bytes 147464 | tf_op jit(solution)/shard_map/ppermute | solution.py:17
  231.4 19.7 %collective-permute-start.17 = (f32[1,1,3,32,128]{4,2,3,1,0:T(4,128)S(1)}, f32[1,1,3,32,128]{4,2,3,1,0:T(4,128)S(1)}, u32[]{:S(2)}, u32[]{:S(2)}) collective-permute-start(f32[1,1,3,32,128]{4,2,3,1,0:T(4,128)S(1)} %bitcast.325), channel_id=1, source_target_pairs={{0,8},{4,12},{8,16},{12,20},{16,24},{20,28},{24,32},{28,36},{32,40... | collective-permute-start | bytes 147464 | tf_op jit(solution)/shard_map/ppermute | solution.py:17
  251.3 30.8 %collective-permute-start.22 = (f32[1,1,3,32,128]{4,2,3,1,0:T(4,128)S(1)}, f32[1,1,3,32,128]{4,2,3,1,0:T(4,128)S(1)}, u32[]{:S(2)}, u32[]{:S(2)}) collective-permute-start(f32[1,1,3,32,128]{4,2,3,1,0:T(4,128)S(1)} %bitcast.296), channel_id=1, source_target_pairs={{0,124},{4,0},{8,4},{12,8},{16,12},{20,16},{24,20},{28,24},{32,28}... | collective-permute-start | bytes 147464 | tf_op jit(solution)/shard_map/ppermute | solution.py:17
  253.2 30.8 %collective-permute-start.23 = (f32[1,1,3,32,128]{4,2,3,1,0:T(4,128)S(1)}, f32[1,1,3,32,128]{4,2,3,1,0:T(4,128)S(1)}, u32[]{:S(2)}, u32[]{:S(2)}) collective-permute-start(f32[1,1,3,32,128]{4,2,3,1,0:T(4,128)S(1)} %bitcast.297), channel_id=1, source_target_pairs={{0,120},{4,124},{8,0},{12,4},{16,8},{20,12},{24,16},{28,20},{32,24... | collective-permute-start | bytes 147464 | tf_op jit(solution)/shard_map/ppermute | solution.py:17
  257.0 39.8 %collective-permute-start.18 = (f32[3,32,128]{2,0,1:T(4,128)S(1)}, f32[3,32,128]{2,0,1:T(4,128)S(1)}, u32[]{:S(2)}, u32[]{:S(2)}) collective-permute-start(f32[3,32,128]{2,0,1:T(4,128)S(1)} %get-tuple-element.442), channel_id=1, source_target_pairs={{0,256},{128,384},{256,512},{384,640},{512,768},{640,896},{768,0},... | collective-permute-start | bytes 147464 | tf_op jit(solution)/shard_map/ppermute | solution.py:17
  258.9 37.9 %collective-permute-start.19 = (f32[3,32,128]{2,0,1:T(4,128)S(1)}, f32[3,32,128]{2,0,1:T(4,128)S(1)}, u32[]{:S(2)}, u32[]{:S(2)}) collective-permute-start(f32[3,32,128]{2,0,1:T(4,128)S(1)} %get-tuple-element.442), channel_id=1, source_target_pairs={{0,128},{128,256},{256,384},{384,512},{512,640},{640,768},{768,896... | collective-permute-start | bytes 147464 | tf_op jit(solution)/shard_map/ppermute | solution.py:17
  260.9 36.0 %collective-permute-start.20 = (f32[3,32,128]{2,0,1:T(4,128)S(1)}, f32[3,32,128]{2,0,1:T(4,128)S(1)}, u32[]{:S(2)}, u32[]{:S(2)}) collective-permute-start(f32[3,32,128]{2,0,1:T(4,128)S(1)} %get-tuple-element.442), channel_id=1, source_target_pairs={{0,896},{128,0},{256,128},{384,256},{512,384},{640,512},{768,640},... | collective-permute-start | bytes 147464 | tf_op jit(solution)/shard_map/ppermute | solution.py:17
  282.1 15.2 %collective-permute-start.21 = (f32[3,32,128]{2,0,1:T(4,128)S(1)}, f32[3,32,128]{2,0,1:T(4,128)S(1)}, u32[]{:S(2)}, u32[]{:S(2)}) collective-permute-start(f32[3,32,128]{2,0,1:T(4,128)S(1)} %get-tuple-element.442), channel_id=1, source_target_pairs={{0,768},{128,896},{256,0},{384,128},{512,256},{640,384},{768,512},... | collective-permute-start | bytes 147464 | tf_op jit(solution)/shard_map/ppermute | solution.py:17
  341.7 58.0 %all-to-all-start.1 = ((f32[4,3,1,3,32,128]{5,4,3,2,1,0:T(8,128)}), f32[4,3,1,3,32,128]{5,4,3,2,1,0:T(8,128)S(1)}, u32[]{:S(2)}, u32[]{:S(2)}) async-start(f32[4,3,1,3,32,128]{5,4,3,2,1,0:T(8,128)} %copy.107), calls=%async_computation.1 | async-start | bytes 1179648 | tf_op jit(solution)/shard_map/all_to_all | solution.py:39
  346.7 63.5 %collective-permute-start.24 = (f32[3,32,128]{2,0,1:T(4,128)S(1)}, f32[3,32,128]{2,0,1:T(4,128)S(1)}, u32[]{:S(2)}, u32[]{:S(2)}) collective-permute-start(f32[3,32,128]{2,0,1:T(4,128)S(1)} %get-tuple-element.462), channel_id=1, source_target_pairs={{0,768},{128,896},{256,0},{384,128},{512,256},{640,384},{768,512},... | collective-permute-start | bytes 147464 | tf_op jit(solution)/shard_map/ppermute | solution.py:17
  380.4 36.3 %collective-permute-start.25 = (f32[3,32,128]{2,0,1:T(4,128)S(1)}, f32[3,32,128]{2,0,1:T(4,128)S(1)}, u32[]{:S(2)}, u32[]{:S(2)}) collective-permute-start(f32[3,32,128]{2,0,1:T(4,128)S(1)} %get-tuple-element.465), channel_id=1, source_target_pairs={{0,896},{128,0},{256,128},{384,256},{512,384},{640,512},{768,640},... | collective-permute-start | bytes 147464 | tf_op jit(solution)/shard_map/ppermute | solution.py:17
  384.9 31.7 %collective-permute-start.26 = (f32[3,32,128]{2,0,1:T(4,128)S(1)}, f32[3,32,128]{2,0,1:T(4,128)S(1)}, u32[]{:S(2)}, u32[]{:S(2)}) collective-permute-start(f32[3,32,128]{2,0,1:T(4,128)S(1)} %get-tuple-element.464), channel_id=1, source_target_pairs={{0,128},{128,256},{256,384},{384,512},{512,640},{640,768},{768,896... | collective-permute-start | bytes 147464 | tf_op jit(solution)/shard_map/ppermute | solution.py:17
  389.9 26.8 %collective-permute-start.27 = (f32[3,32,128]{2,0,1:T(4,128)S(1)}, f32[3,32,128]{2,0,1:T(4,128)S(1)}, u32[]{:S(2)}, u32[]{:S(2)}) collective-permute-start(f32[3,32,128]{2,0,1:T(4,128)S(1)} %get-tuple-element.463), channel_id=1, source_target_pairs={{0,256},{128,384},{256,512},{384,640},{512,768},{640,896},{768,0},... | collective-permute-start | bytes 147464 | tf_op jit(solution)/shard_map/ppermute | solution.py:17
  399.8 16.9 %collective-permute-start.28 = (f32[1,1,3,32,128]{4,2,3,1,0:T(4,128)S(1)}, f32[1,1,3,32,128]{4,2,3,1,0:T(4,128)S(1)}, u32[]{:S(2)}, u32[]{:S(2)}) collective-permute-start(f32[1,1,3,32,128]{4,2,3,1,0:T(4,128)S(1)} %bitcast.324), channel_id=1, source_target_pairs={{0,4},{4,8},{8,12},{12,16},{16,20},{20,24},{24,28},{28,32},{32,36}... | collective-permute-start | bytes 147464 | tf_op jit(solution)/shard_map/ppermute | solution.py:17
  410.2 25.1 %collective-permute-start.29 = (f32[1,1,3,32,128]{4,2,3,1,0:T(4,128)S(1)}, f32[1,1,3,32,128]{4,2,3,1,0:T(4,128)S(1)}, u32[]{:S(2)}, u32[]{:S(2)}) collective-permute-start(f32[1,1,3,32,128]{4,2,3,1,0:T(4,128)S(1)} %bitcast.326), channel_id=1, source_target_pairs={{0,8},{4,12},{8,16},{12,20},{16,24},{20,28},{24,32},{28,36},{32,40... | collective-permute-start | bytes 147464 | tf_op jit(solution)/shard_map/ppermute | solution.py:17
where the time goes:
time: 439 us; the launch traced here: 437 us
  starting transfers between devices  252 us (57%)
  waiting for transfers between devices  62 us (14%)
  other arithmetic  60.1 us (14%)
  local copies, waits for them, and re-layouts  35.9 us (8%)
  blocking collectives  24 us (5%)
    ppermute x30, starting transfers between devices, from_behind(): return lax.ppermute(value, axis, pairs)  243 us
    ppermute x30, waiting for transfers between devices, from_behind(): return lax.ppermute(value, axis, pairs)  62 us
    all_gather x2, blocking collectives, in_one_piece(): result = lax.all_gather(both, axis, axis=dim, tiled=True)  24 us
    reduce_sum x8, other arithmetic, block_forces(): jnp.sum(pair_push, axis=2)  16.5 us
    gather x8, local copies, waits for them, and re-layouts, block_forces(): tower_side = tower_pos[tower_block, :, tower_index, :]  12.7 us
    scatter-add x8, other arithmetic, block_forces(): tower_force.at[tower_block, :, tower_index, :]  10.3 us
    scatter-add x8, other arithmetic, block_forces(): plate_force.at[plate_block, :, plate_index, :]  10.3 us
    all_to_all x2, starting transfers between devices, summed_on_arrival(): lax.all_to_all(in_blocks(value, dim, count), axis, 0, 0, tiled=True)  8.97 us
  transfers between devices with their start and end apart: 32, of which 8 were waited for; matrix products, arithmetic and copies ran while one was open for 2% of the time, Pallas kernels for 0%

commit v1 on v0

v1 whole, which is shorter than its diff:
```python
import functools

import jax
import jax.numpy as jnp
from jax import lax
from jax.experimental import pallas as pl
from jax.experimental.pallas import tpu as pltpu
from jax.sharding import PartitionSpec as P

time_step = 0.02
CL = 32
CS = 128
PAIRS = 128
GROUP = 8
MESH = pl.DeviceIdType.MESH
COPIES = 32
F32 = jnp.float32
BF16 = jnp.bfloat16


def rounded(v):
    return v.astype(BF16).astype(F32)


def split3(v):
    a = rounded(v)
    r = v - a
    b = rounded(r)
    return a, b, rounded(r - b)


def features(rows, weight, sub):
    sq = rows * rows
    norm = (sq[0:1] + sq[1:2] + sq[2:3]) * 0.25
    scaled = rows * weight
    high = rounded(scaled)
    sums = jnp.concatenate([high, scaled - high], axis=0).astype(BF16)
    return norm, sums


def gather_side(pos, wts, block, index, shift, sub):
    x = jnp.broadcast_to(pos[block, 0, pl.ds(index, 1), :], (8, CS))
    y = jnp.broadcast_to(pos[block, 1, pl.ds(index, 1), :], (8, CS))
    z = jnp.broadcast_to(pos[block, 2, pl.ds(index, 1), :], (8, CS))
    s = jnp.broadcast_to(wts[block, 3, pl.ds(index, 1), :], (8, CS))
    one = jnp.where(sub == 3, 1.0, 0.0)
    rows = jnp.where(sub == 0, x, jnp.where(sub == 1, y, jnp.where(sub == 2, z, one)))
    if shift is not None:
        rows = rows + shift
    return rows, s


def one_pair(n, tower, wt_tower, plate, wt_plate, t_slots, p_slots, height, sub):
    ts = t_slots[0, n]
    ps = p_slots[0, n]
    t_block = lax.shift_right_logical(ts, 5)
    t_index = lax.bitwise_and(ts, 31)
    p_block = lax.shift_right_logical(ps, 5)
    p_index = lax.bitwise_and(ps, 31)
    dx = (t_block - 2).astype(F32)
    dy = -lax.shift_right_logical(ps, 7).astype(F32)
    dz = (height - lax.bitwise_and(p_block, 3)).astype(F32)
    shift = jnp.where(sub == 0, dx, jnp.where(sub == 1, dy, jnp.where(sub == 2, dz, 0.0)))
    a, sa = gather_side(tower, wt_tower, t_block, t_index, shift, sub)
    q, sq = gather_side(plate, wt_plate, p_block, p_index, None, sub)
    norm_a, sums_a = features(a, sa, sub)
    norm_q, sums_q = features(q, sq, sub)
    left = jnp.where(
        sub < 3, 0.5 * a, jnp.where(sub == 3, 1.0 - norm_a, jnp.where(sub == 4, 1.0, 0.0))
    )
    right = jnp.where(sub == 4, -norm_q, q)
    a1, a2, a3 = split3(left)
    q1, q2, q3 = split3(right)
    lhs = jnp.concatenate([a1, a1, a2, a1, a3, a2], axis=0)
    rhs = jnp.concatenate([q1, q2, q1, q3, q1, q2], axis=0)
    return dict(a=a, sa=sa, q=q, sq=sq, sums_a=sums_a, sums_q=sums_q, lhs=lhs, rhs=rhs)


def dot(a, b, dims):
    return lax.dot_general(a, b, (dims, ((), ())), preferred_element_type=F32)


def two_pairs(first, n, fa_ref, fq_ref):
    u, v = first
    lhs = jnp.concatenate([u["lhs"], v["lhs"]], axis=0)
    lhs = lhs.T.astype(BF16)
    zero = jnp.zeros((48, CS), F32)
    rhs = jnp.concatenate(
        [jnp.concatenate([u["rhs"], zero], axis=1), jnp.concatenate([zero, v["rhs"]], axis=1)],
        axis=0,
    ).astype(BF16)
    t = dot(lhs, rhs, ((1,), (0,)))
    m = jnp.maximum(t, 0.0)
    m = (m * m).astype(BF16)
    wa = jnp.concatenate([u["sums_a"], v["sums_a"]], axis=0)
    wq = jnp.concatenate([u["sums_q"], v["sums_q"]], axis=0)
    on_q = dot(wa, m, ((1,), (0,)))
    stacked = jnp.concatenate([m[:, :CS], m[:, CS:]], axis=0)
    on_a = dot(wq, stacked, ((1,), (1,)))
    for k, w in enumerate((u, v)):
        cols = slice(k * CS, (k + 1) * CS)
        for rows, weight, out, ref in (
            (w["a"], w["sa"], on_a, fa_ref),
            (w["q"], w["sq"], on_q, fq_ref),
        ):
            got = out[16 * k : 16 * k + 8, cols] + out[16 * k + 8 : 16 * k + 16, cols]
            force = (rows * got[3:4] - got) * (4.0 * weight)
            for c in range(3):
                ref[c, pl.ds(n + k, 1), :] = force[c : c + 1]


def spread(pair_forces, slots, live, count, out_ref, blocks):
    rows = blocks * CL
    which = lax.broadcasted_iota(jnp.int32, (rows, PAIRS), 0)
    pick = jnp.where((which == slots) & (live < count), 1.0, 0.0).astype(BF16)
    pick = jnp.concatenate([pick, pick], axis=1)
    for c in range(3):
        v = pair_forces[c]
        high = rounded(v)
        both = jnp.concatenate([high, v - high], axis=0).astype(BF16)
        out_ref[:, c] = dot(pick, both, ((1,), (0,))).reshape(blocks, CL, CS)


def kernel(
    pos_ref, vel_ref, str_ref, ts_ref, ps_ref, cnt_ref, tv_ref, pv_ref,
    out_pos, out_vel,
    plate0, plate1, tower0, tower1, pf0, pf1, tf0, tf1, rt0, rt1, rd0, rd1, rx0, rx1,
    line0, line1, rl0, rl1, fa_ref, fq_ref, now, send, recv,
):
    i = lax.axis_index("gx")
    j = lax.axis_index("gy")
    k = lax.axis_index("gz")
    nx, ny, nz = lax.axis_size("gx"), lax.axis_size("gy"), lax.axis_size("gz")
    core = lax.rem(j, 2)
    at_x = lambda d: {"gx": lax.rem(i + d + nx, nx)}
    at_y = lambda d: {"gy": lax.rem(j + d + ny, ny)}
    at_z = lambda d: {"gz": lax.rem(k + d + nz, nz)}
    partner = {"gy": j + 1 - 2 * core}

    barrier = pltpu.get_barrier_semaphore()
    peers = [at_x(d) for d in (-2, -1, 1, 2)] + [at_y(-2), at_y(2), partner]
    peers += [at_z(d) for d in (1, 2, 3)]
    for peer in peers:
        pl.semaphore_signal(barrier, inc=1, device_id=peer, device_id_type=MESH)

    plate0[k, 0:3] = pos_ref[...]
    plate0[k, 3] = str_ref[...]
    tower0[2, 0:3] = pos_ref[...]
    tower0[2, 3] = str_ref[...]
    now[0] = pos_ref[...]
    now[1] = vel_ref[...]
    pl.semaphore_wait(barrier, len(peers))

    sub = lax.broadcasted_iota(jnp.int32, (8, CS), 0)
    live = lax.broadcasted_iota(jnp.int32, (1, PAIRS), 1)
    count = cnt_ref[0, 0]
    started = []

    def push(leap, number, src, dst, where):
        copy = pltpu.make_async_remote_copy(
            src_ref=src, dst_ref=dst,
            send_sem=send.at[leap, number], recv_sem=recv.at[leap, number],
            device_id=where, device_id_type=MESH,
        )
        copy.start()
        started.append(copy)
        return copy

    for leap in range(2):
        plate, tower = ((plate0, tower0), (plate1, tower1))[leap]
        pf, tf = ((pf0, tf0), (pf1, tf1))[leap]
        rt, rd, rx = ((rt0, rd0, rx0), (rt1, rd1, rx1))[leap]
        line, rl = ((line0, rl0), (line1, rl1))[leap]
        go = functools.partial(push, leap)

        line_in = go(0, plate.at[k], plate.at[2 * nz + k], at_y(-2))
        tower_in = [
            go(1 + s, plate.at[k], tower.at[2 + d], at_x(-d)) for s, d in enumerate((-2, 2, -1, 1))
        ]
        own_in = [go(5 + r, plate.at[k], plate.at[k], at_z(r)) for r in (1, 2, 3)]
        source = 2 * nz * (1 - core)

        height = lambda r: lax.rem(k - r + nz, nz)

        def share_if(who, r, plate=plate, leap=leap):
            @pl.when(core == who)
            def _():
                pltpu.make_async_remote_copy(
                    src_ref=plate.at[source + height(r)], dst_ref=plate.at[nz + height(r)],
                    send_sem=send.at[leap, 12 + r], recv_sem=recv.at[leap, 12 + r],
                    device_id=partner, device_id_type=MESH,
                ).start()

        share_if(1, 0)
        for r in (1, 2, 3):
            own_in[r - 1].wait_recv()
            share_if(1, r)
        line_in.wait_recv()
        far_in = [go(8 + r, plate.at[2 * nz + k], plate.at[2 * nz + k], at_z(r)) for r in (1, 2, 3)]
        share_if(0, 0)
        for r in (1, 2, 3):
            far_in[r - 1].wait_recv()
            share_if(0, r)
        for r in range(4):
            copy = pltpu.make_async_remote_copy(
                src_ref=plate.at[source + height(r)], dst_ref=plate.at[nz + height(r)],
                send_sem=send.at[leap, 12 + r], recv_sem=recv.at[leap, 12 + r],
                device_id=partner, device_id_type=MESH,
            )
            started.append(copy)
            copy.wait_recv()
        for copy in tower_in:
            copy.wait_recv()

        def pairs(g, carry, tower=tower, plate=plate):
            base = g * GROUP
            for two in range(GROUP // 2):
                n = base + 2 * two
                both = [
                    one_pair(n + w, tower, tower0, plate, plate0, ts_ref, ps_ref, k, sub)
                    for w in range(2)
                ]
                two_pairs(both, n, fa_ref, fq_ref)
            return carry

        lax.fori_loop(0, PAIRS // GROUP, pairs, 0)
        spread(fq_ref, pv_ref[...], live, count, pf, 3 * 4)
        spread(fa_ref, tv_ref[...], live, count, tf, 5)

        mid = go(16, pf.at[pl.ds(nz, nz)], rd, partner)
        rows_in = [
            go(17 + s, tf.at[2 + d], rt.at[s], at_x(d)) for s, d in enumerate((-2, 2, -1, 1))
        ]
        first = 2 * nz * core
        second = 2 * nz * (1 - core)
        early = [
            go(20 + r, pf.at[first + lax.rem(k + r, nz)], rx.at[r - 1], at_z(r)) for r in (1, 2, 3)
        ]
        mid.wait_recv()
        pf[pl.ds(second, nz)] = pf[pl.ds(second, nz)] + rd[...]
        late = [
            go(23 + r, pf.at[second + lax.rem(k + r, nz)], rx.at[2 + r], at_z(r))
            for r in (1, 2, 3)
        ]
        for copy in early:
            copy.wait_recv()
        sum_early = pf[first + k] + rx[0] + rx[1] + rx[2]
        for copy in late:
            copy.wait_recv()
        sum_late = pf[second + k] + rx[3] + rx[4] + rx[5]
        is_even = core == 0
        line[...] = jnp.where(is_even, sum_late, sum_early)
        home = go(27, line, rl, at_y(2))
        force = jnp.where(is_even, sum_early, sum_late) + tf[2]
        for copy in rows_in:
            copy.wait_recv()
        force = force + rt[0] + rt[1] + rt[2] + rt[3]
        home.wait_recv()
        force = force + rl[...]
        speed = now[1] + time_step * force
        place = now[0] + time_step * speed
        if leap == 0:
            now[1] = speed
            now[0] = place
            plate1[k] = place
            tower1[2] = place
        else:
            out_vel[...] = speed
            out_pos[...] = place
    for copy in started:
        copy.wait_send()


def shards(positions, velocities, strength, tower_slots, plate_slots, pair_count):
    vm = pl.BlockSpec(memory_space=pltpu.VMEM)
    sm = pl.BlockSpec(memory_space=pltpu.SMEM)
    block = (3, CL, CS)
    scratch = []
    for shape in ((12, 4, CL, CS), (12, *block), (5, 4, CL, CS), (5, *block)):
        scratch.append(pltpu.VMEM(shape, F32))
    for blocks in (12, 5, 4, 4, 6):
        scratch += [pltpu.VMEM((blocks, *block), F32)] * 2
    scratch += [pltpu.VMEM(block, F32)] * 4
    scratch += [pltpu.VMEM((3, PAIRS, CS), F32)] * 2
    scratch += [pltpu.VMEM((2, *block), F32)]
    scratch += [pltpu.SemaphoreType.DMA((2, COPIES))] * 2
    tower_slots = tower_slots.reshape(1, PAIRS)
    plate_slots = plate_slots.reshape(1, PAIRS)
    new_pos, new_vel = pl.pallas_call(
        kernel,
        out_shape=[jax.ShapeDtypeStruct(block, F32)] * 2,
        in_specs=[vm, vm, vm, sm, sm, sm, vm, vm],
        out_specs=[vm, vm],
        scratch_shapes=scratch,
        compiler_params=pltpu.CompilerParams(collective_id=0, has_side_effects=True),
        name="leapfrog",
    )(
        positions.reshape(block), velocities.reshape(block), strength.reshape(CL, CS),
        tower_slots, plate_slots, pair_count.reshape(1, 1), tower_slots, plate_slots,
    )
    return new_pos[None, None, None], new_vel[None, None, None]


def solution(mesh):
    wide = P("gx", "gy", "gz", None, None, None)
    in_specs = (
        wide, wide, P("gx", "gy", "gz", None, None),
        P("gx", "gy", "gz", None), P("gx", "gy", "gz", None), P("gx", "gy", "gz"),
    )
    return jax.shard_map(
        shards, mesh=mesh, in_specs=in_specs, out_specs=(wide, wide), check_vma=False
    )
```

time: 439 us -> 137 us (0.31)
  the two profiles are of different devices: /device:TPU:71 before, /device:TPU:64 now
where the time goes in v1:
time: 137 us
  Pallas kernels  133 us (97%)
  local copies, waits for them, and re-layouts  2.06 us (2%)
    pallas_call x1, Pallas kernels, shards(): pl.pallas_call(kernel, out_shape=[jax.ShapeDtypeStruct(block, F32)] * 2,...  133 us

profile of v1, /device:TPU:64, one launch (start us, length us, event | category | flops | bytes accessed | tf_op | source)
XLA Modules:
  0.0 136.7 jit_solution(10731613788650573130)
XLA Ops:
  1.3 133.3 %leapfrog.1 = (f32[3,32,128]{2,1,0:T(8,128)}, f32[3,32,128]{2,1,0:T(8,128)}) custom-call(f32[3,32,128]{2,1,0:T(8,128)} %bitcast.9, f32[3,32,128]{2,1,0:T(8,128)} %bitcast.10, f32[32,128]{1,0:T(8,128)} %bitcast.13, s32[1,128]{1,0:T(1,128)} %bitcast.14, s32[1,128]{1,0:T(1,128)} %bitcast.16, s32[1,1]{1,0:T(1,128)} %bitcast.8.cnt_ref, s32[1,128]{1,0:T(1,128)} %bitcast.15, ...), custom_call_target="tpu_custom_call" | custom-call | tf_op jit(solution)/shard_map/leapfrog/pallas_call | solution.py:289
  134.6 0.0 copy-start
  134.6 1.4 %copy.11 = f32[1,1,1,3,32,128]{5,4,3,2,1,0:T(8,128)} copy(f32[1,1,1,3,32,128]{5,4,3,2,1,0:T(8,128)} %bitcast.12) | data formatting | bytes 98304
  136.1 0.0 copy-done
  136.1 0.6 copy.12
Async XLA Ops:
  134.6 1.4 %copy-start = (f32[3,32,128]{2,1,0:T(8,128)S(1)}, f32[3,32,128]{2,1,0:T(8,128)}, u32[]{:S(2)}) copy-start(f32[3,32,128]{2,1,0:T(8,128)} %get-tuple-element.5) | copy-start | bytes 147460

commit v2 on v1

v2 whole, which is shorter than its diff:
```python
import jax
import jax.numpy as jnp
from jax import lax
from jax.experimental import pallas as pl
from jax.experimental.pallas import tpu as pltpu
from jax.sharding import PartitionSpec as P

time_step = 0.02
CL = 32
CS = 128
PAIRS = 128
GROUP = 32
PARTS = 2
ROWS = CL // PARTS
MESH = pl.DeviceIdType.MESH
COPIES = 28
F32 = jnp.float32
BF16 = jnp.bfloat16


def rounded(v):
    return v.astype(BF16).astype(F32)


def split3(v):
    a = rounded(v)
    r = v - a
    b = rounded(r)
    return a, b, rounded(r - b)


def features(rows, weight, sub):
    sq = rows * rows
    norm = (sq[0:1] + sq[1:2] + sq[2:3]) * 0.25
    scaled = rows * weight
    high = rounded(scaled)
    sums = jnp.concatenate([high, scaled - high], axis=0).astype(BF16)
    return norm, sums


def gather_side(pos, wts, block, index, shift, sub):
    x = jnp.broadcast_to(pos[block, 0, pl.ds(index, 1), :], (8, CS))
    y = jnp.broadcast_to(pos[block, 1, pl.ds(index, 1), :], (8, CS))
    z = jnp.broadcast_to(pos[block, 2, pl.ds(index, 1), :], (8, CS))
    s = jnp.broadcast_to(wts[block, 3, pl.ds(index, 1), :], (8, CS))
    one = jnp.where(sub == 3, 1.0, 0.0)
    rows = jnp.where(sub == 0, x, jnp.where(sub == 1, y, jnp.where(sub == 2, z, one)))
    if shift is not None:
        rows = rows + shift
    return rows, s


def one_pair(n, tower, wt_tower, plate, wt_plate, t_slots, p_slots, height, sub):
    ts = t_slots[0, n]
    ps = p_slots[0, n]
    t_block = lax.shift_right_logical(ts, 5)
    t_index = lax.bitwise_and(ts, 31)
    p_block = lax.shift_right_logical(ps, 5)
    p_index = lax.bitwise_and(ps, 31)
    dx = (t_block - 2).astype(F32)
    dy = -lax.shift_right_logical(ps, 7).astype(F32)
    dz = (height - lax.bitwise_and(p_block, 3)).astype(F32)
    shift = jnp.where(sub == 0, dx, jnp.where(sub == 1, dy, jnp.where(sub == 2, dz, 0.0)))
    a, sa = gather_side(tower, wt_tower, t_block, t_index, shift, sub)
    q, sq = gather_side(plate, wt_plate, p_block, p_index, None, sub)
    norm_a, sums_a = features(a, sa, sub)
    norm_q, sums_q = features(q, sq, sub)
    left = jnp.where(
        sub < 3, 0.5 * a, jnp.where(sub == 3, 1.0 - norm_a, jnp.where(sub == 4, 1.0, 0.0))
    )
    right = jnp.where(sub == 4, -norm_q, q)
    a1, a2, a3 = split3(left)
    q1, q2, q3 = split3(right)
    lhs = jnp.concatenate([a1, a1, a2, a1, a3, a2], axis=0)
    rhs = jnp.concatenate([q1, q2, q1, q3, q1, q2], axis=0)
    return dict(a=a, sa=sa, q=q, sq=sq, sums_a=sums_a, sums_q=sums_q, lhs=lhs, rhs=rhs)


def dot(a, b, dims):
    return lax.dot_general(a, b, (dims, ((), ())), preferred_element_type=F32)


def beside(u, v):
    lhs = jnp.concatenate([u["lhs"], v["lhs"]], axis=0).T.astype(BF16)
    zero = jnp.zeros((48, CS), F32)
    rhs = jnp.concatenate(
        [jnp.concatenate([u["rhs"], zero], axis=1), jnp.concatenate([zero, v["rhs"]], axis=1)],
        axis=0,
    ).astype(BF16)
    return lhs, rhs


def group_of_pairs(sides, n, fa_ref, fq_ref):
    twos = [sides[w : w + 2] for w in range(0, len(sides), 2)]
    products = [beside(u, v) for u, v in twos]
    ts = [dot(lhs, rhs, ((1,), (0,))) for lhs, rhs in products]
    outs = []
    for (u, v), t in zip(twos, ts):
        m = jnp.maximum(t, 0.0)
        m = (m * m).astype(BF16)
        wa = jnp.concatenate([u["sums_a"], v["sums_a"]], axis=0)
        wq = jnp.concatenate([u["sums_q"], v["sums_q"]], axis=0)
        stacked = jnp.concatenate([m[:, :CS], m[:, CS:]], axis=0)
        outs.append((dot(wq, stacked, ((1,), (1,))), dot(wa, m, ((1,), (0,)))))
    for w, side in enumerate(sides):
        half = w % 2
        cols = slice(half * CS, (half + 1) * CS)
        on_a, on_q = outs[w // 2]
        for rows, weight, out, ref in (
            (side["a"], side["sa"], on_a, fa_ref),
            (side["q"], side["sq"], on_q, fq_ref),
        ):
            got = out[16 * half : 16 * half + 8, cols] + out[16 * half + 8 : 16 * half + 16, cols]
            force = (rows * got[3:4] - got) * (4.0 * weight)
            for c in range(3):
                ref[c, pl.ds(n + w, 1), :] = force[c : c + 1]


def spread(pair_forces, slots, live, count, out_ref, blocks):
    rows = blocks * CL
    which = lax.broadcasted_iota(jnp.int32, (rows, PAIRS), 0)
    pick = jnp.where((which == slots) & (live < count), 1.0, 0.0).astype(BF16)
    pick = jnp.concatenate([pick, pick], axis=1)
    for c in range(3):
        v = pair_forces[c]
        high = rounded(v)
        both = jnp.concatenate([high, v - high], axis=0).astype(BF16)
        out_ref[:, c] = dot(pick, both, ((1,), (0,))).reshape(blocks, CL, CS)


def kernel(
    pos_ref, vel_ref, str_ref, ts_ref, ps_ref, cnt_ref, tv_ref, pv_ref,
    out_pos, out_vel,
    plate0, plate1, tower0, tower1, pf0, pf1, tf0, tf1, rt0, rt1, rd0, rd1, rx0, rx1,
    line0, line1, rl0, rl1, fa_ref, fq_ref, now, send, recv,
):
    i = lax.axis_index("gx")
    j = lax.axis_index("gy")
    k = lax.axis_index("gz")
    nx, ny, nz = lax.axis_size("gx"), lax.axis_size("gy"), lax.axis_size("gz")
    core = lax.rem(j, 2)
    at_x = lambda d: {"gx": lax.rem(i + d + nx, nx)}
    at_y = lambda d: {"gy": lax.rem(j + d + ny, ny)}
    at_z = lambda d: {"gz": lax.rem(k + d + nz, nz)}
    partner = {"gy": j + 1 - 2 * core}
    steps = ((0, -2), (1, 2), (2, -1), (3, 1))

    barrier = pltpu.get_barrier_semaphore()
    peers = [at_x(d) for d in (-2, -1, 1, 2)] + [at_y(-2), at_y(2), partner]
    peers += [at_z(d) for d in (1, 2, 3)]
    for peer in peers:
        pl.semaphore_signal(barrier, inc=1, device_id=peer, device_id_type=MESH)

    plate0[k, 0:3] = pos_ref[...]
    plate0[k, 3] = str_ref[...]
    tower0[2, 0:3] = pos_ref[...]
    tower0[2, 3] = str_ref[...]
    now[0] = pos_ref[...]
    now[1] = vel_ref[...]
    with jax.named_scope("barrier"):
        pl.semaphore_wait(barrier, len(peers))

    sub = lax.broadcasted_iota(jnp.int32, (8, CS), 0)
    live = lax.broadcasted_iota(jnp.int32, (1, PAIRS), 1)
    count = cnt_ref[0, 0]
    started = []

    def copy_of(leap, part, number, src, dst, where):
        return pltpu.make_async_remote_copy(
            src_ref=src, dst_ref=dst,
            send_sem=send.at[leap, part, number], recv_sem=recv.at[leap, part, number],
            device_id=where, device_id_type=MESH,
        )

    def go(*args):
        copy = copy_of(*args)
        copy.start()
        started.append(copy)
        return copy

    def rows(part):
        return pl.ds(part * ROWS, ROWS)

    def await_all(copies, name):
        for copy in copies:
            with jax.named_scope(name):
                copy.wait_recv()

    def send_line(leap, part, plate):
        r = rows(part)
        return go(leap, part, 0, plate.at[k, :, r], plate.at[2 * nz + k, :, r], at_y(-2))

    def send_tower(leap, part, plate, tower):
        r = rows(part)
        return [
            go(leap, part, 1 + s, plate.at[k, :, r], tower.at[2 + d, :, r], at_x(-d))
            for s, d in steps
        ]

    def send_over(leap, part, plate, number, block):
        r = rows(part)
        return [
            go(leap, part, number + d, plate.at[block, :, r], plate.at[block, :, r], at_z(d + 1))
            for d in range(3)
        ]

    def shared(leap, part, plate, d):
        height = lax.rem(k - d + nz, nz)
        r = rows(part)
        return copy_of(
            leap, part, 11 + d,
            plate.at[2 * nz * (1 - core) + height, :, r], plate.at[nz + height, :, r], partner,
        )

    def share_if(who, *args):
        @pl.when(core == who)
        def _():
            shared(*args).start()

    parts = range(PARTS)
    line_in = [send_line(0, part, plate0) for part in parts]
    own_in = [send_over(0, part, plate0, 5, k) for part in parts]
    tower_in = [send_tower(0, part, plate0, tower0) for part in parts]
    for leap in range(2):
        plate, tower = ((plate0, tower0), (plate1, tower1))[leap]
        pf, tf = ((pf0, tf0), (pf1, tf1))[leap]
        rt, rd, rx = ((rt0, rd0, rx0), (rt1, rd1, rx1))[leap]
        line, rl = ((line0, rl0), (line1, rl1))[leap]

        for part in parts:
            share_if(1, leap, part, plate, 0)
            for d in range(3):
                await_all([own_in[part][d]], f"own{leap}")
                share_if(1, leap, part, plate, d + 1)
        far_in = []
        for part in parts:
            await_all([line_in[part]], f"line{leap}")
            far_in.append(send_over(leap, part, plate, 8, 2 * nz + k))
            share_if(0, leap, part, plate, 0)
        for part in parts:
            for d in range(3):
                await_all([far_in[part][d]], f"far{leap}")
                share_if(0, leap, part, plate, d + 1)
        between = [shared(leap, part, plate, d) for part in parts for d in range(nz)]
        started += between
        await_all(between, f"mid{leap}")
        for part in parts:
            await_all(tower_in[part], f"tower{leap}")

        def pairs(g, carry, tower=tower, plate=plate):
            base = g * GROUP
            sides = [
                one_pair(base + w, tower, tower0, plate, plate0, ts_ref, ps_ref, k, sub)
                for w in range(GROUP)
            ]
            group_of_pairs(sides, base, fa_ref, fq_ref)
            return carry

        with jax.named_scope(f"pairs{leap}"):
            lax.fori_loop(0, PAIRS // GROUP, pairs, 0)
        with jax.named_scope(f"spread{leap}"):
            spread(fq_ref, pv_ref[...], live, count, pf, 3 * 4)
            spread(fa_ref, tv_ref[...], live, count, tf, 5)

        first = 2 * nz * core
        second = 2 * nz * (1 - core)

        def over(part, number, block, slot, leap=leap, pf=pf, rx=rx):
            r = rows(part)
            return [
                go(
                    leap, part, number + d, pf.at[block + lax.rem(k + d + 1, nz), :, r],
                    rx.at[slot + d, :, r], at_z(d + 1),
                )
                for d in range(3)
            ]

        mid, early, rows_in, late, home = [], [], [], [], []
        for part in parts:
            r = rows(part)
            mid.append(go(leap, part, 15, pf.at[pl.ds(nz, nz), :, r], rd.at[:, :, r], partner))
            early.append(over(part, 20, first, 0))
            rows_in.append([
                go(leap, part, 16 + s, tf.at[2 + d, :, r], rt.at[s, :, r], at_x(d))
                for s, d in steps
            ])
        for part in parts:
            r = rows(part)
            await_all([mid[part]], f"rmid{leap}")
            pf[pl.ds(second, nz), :, r] = pf[pl.ds(second, nz), :, r] + rd[:, :, r]
            late.append(over(part, 23, second, 3))
        keep = []
        for part in parts:
            r = rows(part)
            await_all(early[part], f"early{leap}")
            sum_early = pf[first + k, :, r] + rx[0, :, r] + rx[1, :, r] + rx[2, :, r]
            await_all(late[part], f"late{leap}")
            sum_late = pf[second + k, :, r] + rx[3, :, r] + rx[4, :, r] + rx[5, :, r]
            line[:, r] = jnp.where(core == 0, sum_late, sum_early)
            home.append(go(leap, part, 26, line.at[:, r], rl.at[:, r], at_y(2)))
            keep.append(jnp.where(core == 0, sum_early, sum_late) + tf[2, :, r])
        line_in, own_in, tower_in = [], [], []
        for part in parts:
            r = rows(part)
            await_all(rows_in[part], f"rrows{leap}")
            force = keep[part] + rt[0, :, r] + rt[1, :, r] + rt[2, :, r] + rt[3, :, r]
            await_all([home[part]], f"home{leap}")
            force = force + rl[:, r]
            speed = now[1, :, r] + time_step * force
            place = now[0, :, r] + time_step * speed
            if leap == 0:
                now[1, :, r] = speed
                now[0, :, r] = place
                plate1[k, :, r] = place
                tower1[2, :, r] = place
                line_in.append(send_line(1, part, plate1))
                own_in.append(send_over(1, part, plate1, 5, k))
                tower_in.append(send_tower(1, part, plate1, tower1))
            else:
                out_vel[:, r] = speed
                out_pos[:, r] = place
    with jax.named_scope("sends"):
        for copy in started:
            copy.wait_send()


def shards(positions, velocities, strength, tower_slots, plate_slots, pair_count):
    vm = pl.BlockSpec(memory_space=pltpu.VMEM)
    sm = pl.BlockSpec(memory_space=pltpu.SMEM)
    block = (3, CL, CS)
    scratch = []
    for shape in ((12, 4, CL, CS), (12, *block), (5, 4, CL, CS), (5, *block)):
        scratch.append(pltpu.VMEM(shape, F32))
    for blocks in (12, 5, 4, 4, 6):
        scratch += [pltpu.VMEM((blocks, *block), F32)] * 2
    scratch += [pltpu.VMEM(block, F32)] * 4
    scratch += [pltpu.VMEM((3, PAIRS, CS), F32)] * 2
    scratch += [pltpu.VMEM((2, *block), F32)]
    scratch += [pltpu.SemaphoreType.DMA((2, PARTS, COPIES))] * 2
    tower_slots = tower_slots.reshape(1, PAIRS)
    plate_slots = plate_slots.reshape(1, PAIRS)
    new_pos, new_vel = pl.pallas_call(
        kernel,
        out_shape=[jax.ShapeDtypeStruct(block, F32)] * 2,
        in_specs=[vm, vm, vm, sm, sm, sm, vm, vm],
        out_specs=[vm, vm],
        scratch_shapes=scratch,
        compiler_params=pltpu.CompilerParams(collective_id=0, has_side_effects=True),
        name="leapfrog",
    )(
        positions.reshape(block), velocities.reshape(block), strength.reshape(CL, CS),
        tower_slots, plate_slots, pair_count.reshape(1, 1), tower_slots, plate_slots,
    )
    return new_pos[None, None, None], new_vel[None, None, None]


def solution(mesh):
    wide = P("gx", "gy", "gz", None, None, None)
    in_specs = (
        wide, wide, P("gx", "gy", "gz", None, None),
        P("gx", "gy", "gz", None), P("gx", "gy", "gz", None), P("gx", "gy", "gz"),
    )
    return jax.shard_map(
        shards, mesh=mesh, in_specs=in_specs, out_specs=(wide, wide), check_vma=False
    )
```

time: 137 us -> 118 us (0.86)
  the two profiles are of different devices: /device:TPU:64 before, /device:TPU:97 now
where the time goes in v2:
time: 118 us; the launch traced here: 117 us
  Pallas kernels  114 us (97%)
  local copies, waits for them, and re-layouts  2.06 us (2%)
  between operations  1.29 us (1%)
    pallas_call x1, Pallas kernels, shards(): pl.pallas_call(kernel, out_shape=[jax.ShapeDtypeStruct(block, F32)] * 2,...  114 us

profile of v2, /device:TPU:97, one launch (start us, length us, event | category | flops | bytes accessed | tf_op | source)
XLA Modules:
  0.0 117.3 jit_solution(13513371698828241917)
XLA Ops:
  1.3 114.0 %leapfrog.1 = (f32[3,32,128]{2,1,0:T(8,128)}, f32[3,32,128]{2,1,0:T(8,128)}) custom-call(f32[3,32,128]{2,1,0:T(8,128)} %bitcast.9, f32[3,32,128]{2,1,0:T(8,128)} %bitcast.10, f32[32,128]{1,0:T(8,128)} %bitcast.13, s32[1,128]{1,0:T(1,128)} %bitcast.14, s32[1,128]{1,0:T(1,128)} %bitcast.16, s32[1,1]{1,0:T(1,128)} %bitcast.8.cnt_ref, s32[1,128]{1,0:T(1,128)} %bitcast.15, ...), custom_call_target="tpu_custom_call" | custom-call | tf_op jit(solution)/shard_map/leapfrog/pallas_call | solution.py:342
  115.3 0.0 copy-start
  115.3 1.4 %copy.11 = f32[1,1,1,3,32,128]{5,4,3,2,1,0:T(8,128)} copy(f32[1,1,1,3,32,128]{5,4,3,2,1,0:T(8,128)} %bitcast.12) | data formatting | bytes 98304
  116.7 0.0 copy-done
  116.7 0.6 copy.12
Async XLA Ops:
  115.3 1.4 %copy-start = (f32[3,32,128]{2,1,0:T(8,128)S(1)}, f32[3,32,128]{2,1,0:T(8,128)}, u32[]{:S(2)}) copy-start(f32[3,32,128]{2,1,0:T(8,128)} %get-tuple-element.5) | copy-start | bytes 147460

commit v3 on v2

--- a/solution.py
+++ b/solution.py
@@ -13,7 +13,7 @@
 PARTS = 2
 ROWS = CL // PARTS
 MESH = pl.DeviceIdType.MESH
-COPIES = 28
+COPIES = 32
 F32 = jnp.float32
 BF16 = jnp.bfloat16
 
@@ -132,24 +132,32 @@
     pos_ref, vel_ref, str_ref, ts_ref, ps_ref, cnt_ref, tv_ref, pv_ref,
     out_pos, out_vel,
     plate0, plate1, tower0, tower1, pf0, pf1, tf0, tf1, rt0, rt1, rd0, rd1, rx0, rx1,
-    line0, line1, rl0, rl1, fa_ref, fq_ref, now, send, recv,
+    line0, line1, rl0, rl1, fa_ref, fq_ref, now, total, send, recv,
 ):
     i = lax.axis_index("gx")
     j = lax.axis_index("gy")
     k = lax.axis_index("gz")
     nx, ny, nz = lax.axis_size("gx"), lax.axis_size("gy"), lax.axis_size("gz")
+    last = nx - 1
     core = lax.rem(j, 2)
+    back = lax.rem(j - 2 + ny, ny)
+    on = lax.rem(j + 2, ny)
     at_x = lambda d: {"gx": lax.rem(i + d + nx, nx)}
-    at_y = lambda d: {"gy": lax.rem(j + d + ny, ny)}
     at_z = lambda d: {"gz": lax.rem(k + d + nz, nz)}
     partner = {"gy": j + 1 - 2 * core}
-    steps = ((0, -2), (1, 2), (2, -1), (3, 1))
+    is_first, is_second = i == 0, i == 1
+    inner = (i >= 1) & (i <= last - 1)
+    is_late = i >= last - 1
 
     barrier = pltpu.get_barrier_semaphore()
-    peers = [at_x(d) for d in (-2, -1, 1, 2)] + [at_y(-2), at_y(2), partner]
+    peers = [at_x(d) for d in (-2, -1, 1, 2)] + [{"gy": back}, {"gy": on}, partner]
     peers += [at_z(d) for d in (1, 2, 3)]
+
+    def greet(peer):
+        pl.semaphore_signal(barrier, inc=1, device_id=peer, device_id_type=MESH)
+
     for peer in peers:
-        pl.semaphore_signal(barrier, inc=1, device_id=peer, device_id_type=MESH)
+        greet(peer)
 
     plate0[k, 0:3] = pos_ref[...]
     plate0[k, 3] = str_ref[...]
@@ -165,18 +173,27 @@
     count = cnt_ref[0, 0]
     started = []
 
-    def copy_of(leap, part, number, src, dst, where):
+    def when(cond, what):
+        if cond is None:
+            what()
+        else:
+            pl.when(cond)(what)
+
+    def copy_of(at, number, src, dst, where, to=None):
         return pltpu.make_async_remote_copy(
             src_ref=src, dst_ref=dst,
-            send_sem=send.at[leap, part, number], recv_sem=recv.at[leap, part, number],
+            send_sem=send.at[*at, number], recv_sem=recv.at[*at, number if to is None else to],
             device_id=where, device_id_type=MESH,
         )
 
-    def go(*args):
-        copy = copy_of(*args)
-        copy.start()
-        started.append(copy)
+    def go(*args, cond=None, to=None):
+        copy = copy_of(*args, to=to)
+        when(cond, copy.start)
+        started.append((cond, copy))
         return copy
+
+    def arrived(at, number, ref):
+        copy_of(at, number, ref, ref, partner).wait_recv()
 
     def rows(part):
         return pl.ds(part * ROWS, ROWS)
@@ -186,41 +203,58 @@
             with jax.named_scope(name):
                 copy.wait_recv()
 
-    def send_line(leap, part, plate):
-        r = rows(part)
-        return go(leap, part, 0, plate.at[k, :, r], plate.at[2 * nz + k, :, r], at_y(-2))
-
-    def send_tower(leap, part, plate, tower):
-        r = rows(part)
-        return [
-            go(leap, part, 1 + s, plate.at[k, :, r], tower.at[2 + d, :, r], at_x(-d))
-            for s, d in steps
-        ]
-
-    def send_over(leap, part, plate, number, block):
-        r = rows(part)
-        return [
-            go(leap, part, number + d, plate.at[block, :, r], plate.at[block, :, r], at_z(d + 1))
-            for d in range(3)
-        ]
-
-    def shared(leap, part, plate, d):
+    def send_own(at, plate, tower):
+        r = rows(at[1])
+        own, far = plate.at[k, :, r], plate.at[2 * nz + k, :, r]
+        line = go(at, 0, own, far, {"gy": back})
+        go(at, 6, own, tower.at[0, :, r], {"gx": lax.rem(i + 2, nx)}, cond=is_late, to=1)
+        over = [go(at, 8 + d, own, plate.at[k, :, r], at_z(d + 1)) for d in range(3)]
+        go(at, 1, own, tower.at[3, :, r], at_x(-1), cond=i >= 1, to=3)
+        go(at, 2, own, tower.at[1, :, r], at_x(1), cond=i <= last - 1, to=2)
+        go(at, 3, own, tower.at[4, :, r], at_x(-2), cond=i <= 1, to=4)
+        return line, over
+
+    def pass_on(at, tower, cond, number, slot, sends, to_slot, step, to):
+        row = lambda b: tower.at[b, :, rows(at[1])]
+        copy = copy_of(at, sends, row(slot), row(to_slot), at_x(step), to=to)
+
+        @pl.when(cond)
+        def _():
+            arrived(at, number, row(slot))
+            copy.start()
+
+        started.append((cond, copy))
+
+    def rest_of_tower(leap, tower):
+        with jax.named_scope(f"tower{leap}"):
+            for part in parts:
+                at = (leap, part)
+                for cond, number, slot in (
+                    (is_first | (i >= 2), 1, 0), (is_first | (i == last), 2, 1),
+                    (is_first | (i == last), 3, 3), ((i < last - 1) | (i == last), 4, 4),
+                ):
+
+                    @pl.when(cond)
+                    def _(at=at, number=number, slot=slot, part=part):
+                        arrived(at, number, tower.at[slot, :, rows(part)])
+
+    def send_far(at, plate):
+        far = plate.at[2 * nz + k, :, rows(at[1])]
+        return [go(at, 11 + d, far, far, at_z(d + 1)) for d in range(3)]
+
+    def shared(at, plate, d):
         height = lax.rem(k - d + nz, nz)
-        r = rows(part)
+        r = rows(at[1])
         return copy_of(
-            leap, part, 11 + d,
+            at, 14 + d,
             plate.at[2 * nz * (1 - core) + height, :, r], plate.at[nz + height, :, r], partner,
         )
 
     def share_if(who, *args):
-        @pl.when(core == who)
-        def _():
-            shared(*args).start()
+        when(core == who, lambda: shared(*args).start())
 
     parts = range(PARTS)
-    line_in = [send_line(0, part, plate0) for part in parts]
-    own_in = [send_over(0, part, plate0, 5, k) for part in parts]
-    tower_in = [send_tower(0, part, plate0, tower0) for part in parts]
+    own_in = [send_own((0, part), plate0, tower0) for part in parts]
     for leap in range(2):
         plate, tower = ((plate0, tower0), (plate1, tower1))[leap]
         pf, tf = ((pf0, tf0), (pf1, tf1))[leap]
@@ -228,24 +262,32 @@
         line, rl = ((line0, rl0), (line1, rl1))[leap]
 
         for part in parts:
-            share_if(1, leap, part, plate, 0)
+            share_if(1, (leap, part), plate, 0)
+        for part in parts:
             for d in range(3):
-                await_all([own_in[part][d]], f"own{leap}")
-                share_if(1, leap, part, plate, d + 1)
+                await_all([own_in[part][1][d]], f"own{leap}")
+                share_if(1, (leap, part), plate, d + 1)
+        with jax.named_scope(f"relay{leap}"):
+            for part in parts:
+                pass_on((leap, part), tower, inner, 2, 1, 4, 0, 1, 1)
+                pass_on((leap, part), tower, inner, 3, 3, 5, 4, -1, 4)
         far_in = []
         for part in parts:
-            await_all([line_in[part]], f"line{leap}")
-            far_in.append(send_over(leap, part, plate, 8, 2 * nz + k))
-            share_if(0, leap, part, plate, 0)
+            await_all([own_in[part][0]], f"line{leap}")
+            far_in.append(send_far((leap, part), plate))
+            share_if(0, (leap, part), plate, 0)
+        with jax.named_scope(f"wrap{leap}"):
+            for part in parts:
+                pass_on((leap, part), tower, is_second, 1, 0, 7, 1, -1, 2)
+                pass_on((leap, part), tower, i == last - 1, 4, 4, 7, 3, 1, 3)
         for part in parts:
             for d in range(3):
                 await_all([far_in[part][d]], f"far{leap}")
-                share_if(0, leap, part, plate, d + 1)
-        between = [shared(leap, part, plate, d) for part in parts for d in range(nz)]
-        started += between
+                share_if(0, (leap, part), plate, d + 1)
+        between = [shared((leap, part), plate, d) for part in parts for d in range(nz)]
+        started += [(None, copy) for copy in between]
         await_all(between, f"mid{leap}")
-        for part in parts:
-            await_all(tower_in[part], f"tower{leap}")
+        rest_of_tower(leap, tower)
 
         def pairs(g, carry, tower=tower, plate=plate):
             base = g * GROUP
@@ -262,50 +304,85 @@
             spread(fq_ref, pv_ref[...], live, count, pf, 3 * 4)
             spread(fa_ref, tv_ref[...], live, count, tf, 5)
 
-        first = 2 * nz * core
+        odd, even = core == 1, core == 0
         second = 2 * nz * (1 - core)
 
-        def over(part, number, block, slot, leap=leap, pf=pf, rx=rx):
-            r = rows(part)
+        def over(at, number, block, slot, cond=None, pf=pf, rx=rx):
+            r = rows(at[1])
             return [
                 go(
-                    leap, part, number + d, pf.at[block + lax.rem(k + d + 1, nz), :, r],
-                    rx.at[slot + d, :, r], at_z(d + 1),
+                    at, number + d, pf.at[block + lax.rem(k + d + 1, nz), :, r],
+                    rx.at[slot + d, :, r], at_z(d + 1), cond=cond,
                 )
                 for d in range(3)
             ]
 
-        mid, early, rows_in, late, home = [], [], [], [], []
-        for part in parts:
-            r = rows(part)
-            mid.append(go(leap, part, 15, pf.at[pl.ds(nz, nz), :, r], rd.at[:, :, r], partner))
-            early.append(over(part, 20, first, 0))
-            rows_in.append([
-                go(leap, part, 16 + s, tf.at[2 + d, :, r], rt.at[s, :, r], at_x(d))
-                for s, d in steps
-            ])
-        for part in parts:
-            r = rows(part)
+        mid, far_home, near_home, home, keep = [], [], [], [], []
+        for part in parts:
+            at, r = (leap, part), rows(part)
+            mid.append(go(at, 18, pf.at[pl.ds(nz, nz), :, r], rd.at[:, :, r], partner))
+            over(at, 19, 2 * nz, 0, cond=odd)
+            row = lambda n, ref, r=r: ref.at[n, :, r]
+            go(at, 25, row(4, tf), row(0, rt), at_x(1), cond=i < last - 1)
+            go(at, 26, row(0, tf), row(1, rt), at_x(-1), cond=i >= 2)
+            go(at, 29, row(1, tf), row(4, rt), at_x(1), cond=is_first)
+            go(at, 29, row(3, tf), row(4, rt), at_x(-1), cond=i == last)
+            go(at, 30, row(0, tf), row(5, rt), at_x(-2), cond=is_first)
+            go(at, 30, row(4, tf), row(5, rt), at_x(2), cond=i == last)
+            go(at, 27, row(3, tf), row(2, rt), at_x(1), cond=is_first)
+            go(at, 28, row(1, tf), row(3, rt), at_x(-1), cond=i == last)
+        for part in parts:
+            at, r = (leap, part), rows(part)
             await_all([mid[part]], f"rmid{leap}")
             pf[pl.ds(second, nz), :, r] = pf[pl.ds(second, nz), :, r] + rd[:, :, r]
-            late.append(over(part, 23, second, 3))
-        keep = []
-        for part in parts:
-            r = rows(part)
-            await_all(early[part], f"early{leap}")
-            sum_early = pf[first + k, :, r] + rx[0, :, r] + rx[1, :, r] + rx[2, :, r]
-            await_all(late[part], f"late{leap}")
-            sum_late = pf[second + k, :, r] + rx[3, :, r] + rx[4, :, r] + rx[5, :, r]
-            line[:, r] = jnp.where(core == 0, sum_late, sum_early)
-            home.append(go(leap, part, 26, line.at[:, r], rl.at[:, r], at_y(2)))
-            keep.append(jnp.where(core == 0, sum_early, sum_late) + tf[2, :, r])
-        line_in, own_in, tower_in = [], [], []
-        for part in parts:
-            r = rows(part)
-            await_all(rows_in[part], f"rrows{leap}")
-            force = keep[part] + rt[0, :, r] + rt[1, :, r] + rt[2, :, r] + rt[3, :, r]
+            far_home.append(over(at, 19, 2 * nz, 0, cond=even))
+        for part in parts:
+            near_home.append(over((leap, part), 22, 0, 3))
+        for part in parts:
+            at, r = (leap, part), rows(part)
+            await_all(far_home[part], f"rfar{leap}")
+            line[:, r] = pf[2 * nz + k, :, r] + rx[0, :, r] + rx[1, :, r] + rx[2, :, r]
+            home.append(go(at, 31, line.at[:, r], rl.at[:, r], {"gy": on}))
+
+        def add_and_pass(at, cond, number, got, slot, sends, to_slot, step, tf=tf, rt=rt):
+            r = rows(at[1])
+            copy = copy_of(at, sends, tf.at[slot, :, r], rt.at[to_slot, :, r], at_x(step))
+
+            @pl.when(cond)
+            def _():
+                arrived(at, number, rt.at[got, :, r])
+                tf[slot, :, r] = tf[slot, :, r] + rt[got, :, r]
+                copy.start()
+
+            started.append((cond, copy))
+
+        with jax.named_scope(f"rsum{leap}"):
+            for part in parts:
+                at = (leap, part)
+                add_and_pass(at, is_second, 29, 4, 0, 30, 5, -2)
+                add_and_pass(at, i == last - 1, 29, 4, 4, 30, 5, 2)
+                add_and_pass(at, inner, 25, 0, 3, 27, 2, 1)
+                add_and_pass(at, inner, 26, 1, 1, 28, 3, -1)
+        for part in parts:
+            at, r = (leap, part), rows(part)
+            await_all(near_home[part], f"rnear{leap}")
+            keep.append(pf[k, :, r] + rx[3, :, r] + rx[4, :, r] + rx[5, :, r] + tf[2, :, r])
+        own_in = []
+        for part in parts:
+            at, r = (leap, part), rows(part)
+            total[...] = keep[part]
+            with jax.named_scope(f"rrows{leap}"):
+                for cond, number, slot in (
+                    (i >= 1, 27, 2), (i <= last - 1, 28, 3), ((i <= 1) | is_late, 30, 5)
+                ):
+
+                    @pl.when(cond)
+                    def _(at=at, number=number, slot=slot, r=r, rt=rt):
+                        arrived(at, number, rt.at[slot, :, r])
+                        total[...] = total[...] + rt[slot, :, r]
+
             await_all([home[part]], f"home{leap}")
-            force = force + rl[:, r]
+            force = total[...] + rl[:, r]
             speed = now[1, :, r] + time_step * force
             place = now[0, :, r] + time_step * speed
             if leap == 0:
@@ -313,15 +390,13 @@
                 now[0, :, r] = place
                 plate1[k, :, r] = place
                 tower1[2, :, r] = place
-                line_in.append(send_line(1, part, plate1))
-                own_in.append(send_over(1, part, plate1, 5, k))
-                tower_in.append(send_tower(1, part, plate1, tower1))
+                own_in.append(send_own((1, part), plate1, tower1))
             else:
                 out_vel[:, r] = speed
                 out_pos[:, r] = place
     with jax.named_scope("sends"):
-        for copy in started:
-            copy.wait_send()
+        for cond, copy in started:
+            when(cond, copy.wait_send)
 
 
 def shards(positions, velocities, strength, tower_slots, plate_slots, pair_count):
@@ -331,11 +406,11 @@
     scratch = []
     for shape in ((12, 4, CL, CS), (12, *block), (5, 4, CL, CS), (5, *block)):
         scratch.append(pltpu.VMEM(shape, F32))
-    for blocks in (12, 5, 4, 4, 6):
+    for blocks in (12, 5, 6, 4, 6):
         scratch += [pltpu.VMEM((blocks, *block), F32)] * 2
     scratch += [pltpu.VMEM(block, F32)] * 4
     scratch += [pltpu.VMEM((3, PAIRS, CS), F32)] * 2
-    scratch += [pltpu.VMEM((2, *block), F32)]
+    scratch += [pltpu.VMEM((2, *block), F32), pltpu.VMEM((3, ROWS, CS), F32)]
     scratch += [pltpu.SemaphoreType.DMA((2, PARTS, COPIES))] * 2
     tower_slots = tower_slots.reshape(1, PAIRS)
     plate_slots = plate_slots.reshape(1, PAIRS)

time: 118 us -> 114 us (0.966)
  the two profiles are of different devices: /device:TPU:97 before, /device:TPU:128 now
where the time goes in v3:
time: 114 us; the launch traced here: 113 us
  Pallas kernels  110 us (96%)
  local copies, waits for them, and re-layouts  2.06 us (2%)
  between operations  1.29 us (1%)
    pallas_call x1, Pallas kernels, shards(): pl.pallas_call(kernel, out_shape=[jax.ShapeDtypeStruct(block, F32)] * 2,...  110 us

profile of v3, /device:TPU:128, one launch (start us, length us, event | category | flops | bytes accessed | tf_op | source)
XLA Modules:
  0.0 113.0 jit_solution(13845962358815786363)
XLA Ops:
  1.3 109.6 %leapfrog.1 = (f32[3,32,128]{2,1,0:T(8,128)}, f32[3,32,128]{2,1,0:T(8,128)}) custom-call(f32[3,32,128]{2,1,0:T(8,128)} %bitcast.9, f32[3,32,128]{2,1,0:T(8,128)} %bitcast.10, f32[32,128]{1,0:T(8,128)} %bitcast.13, s32[1,128]{1,0:T(1,128)} %bitcast.14, s32[1,128]{1,0:T(1,128)} %bitcast.16, s32[1,1]{1,0:T(1,128)} %bitcast.8.cnt_ref, s32[1,128]{1,0:T(1,128)} %bitcast.15, ...), custom_call_target="tpu_custom_call" | custom-call | tf_op jit(solution)/shard_map/leapfrog/pallas_call | solution.py:417
  110.9 0.0 copy-start
  110.9 1.4 %copy.11 = f32[1,1,1,3,32,128]{5,4,3,2,1,0:T(8,128)} copy(f32[1,1,1,3,32,128]{5,4,3,2,1,0:T(8,128)} %bitcast.12) | data formatting | bytes 98304
  112.4 0.0 copy-done
  112.4 0.6 copy.12
Async XLA Ops:
  110.9 1.4 %copy-start = (f32[3,32,128]{2,1,0:T(8,128)S(1)}, f32[3,32,128]{2,1,0:T(8,128)}, u32[]{:S(2)}) copy-start(f32[3,32,128]{2,1,0:T(8,128)} %get-tuple-element.5) | copy-start | bytes 147460
